TPU v7x, 128 devices: a whole 4x4x4 slice. The times are simulated.
128 devices in a mesh: gx: 32 (over y, z, core), gy: 4 (over x).
Axes of the slice: x: 4, y: 4, z: 4, core: 2. Of those that a mesh axis runs over, the one named last changes fastest.
Arguments:
- velocity: bfloat16 [3, 64, 16, 16, 512], P(None, 'gx', 'gy'), may hold values from -6 to 6
- part_pos: float32 [16384, 3, 128], P(('gx', 'gy')), may hold values from -1 to 1
- part_vel: float32 [16384, 3, 128], P(('gx', 'gy')), may hold values from -6 to 6
- part_coef: float32 [16384, 2, 128], P(('gx', 'gy')), may hold values from 0.3 to 3
- counts: int32 [16384], P(('gx', 'gy')), may hold values from 1 to 128
- dest: int32 [16384], P(('gx', 'gy')), may hold values from 0 to 3, as said below
- elem: int32 [16384], P(('gx', 'gy')), may hold values from 0 to 127, as said below
Outputs:
- drag: float32 [16384, 3, 128], P(('gx', 'gy'))
- source: float32 [3, 64, 16, 16, 512], P(None, 'gx', 'gy')
Inputs may be any that keep to these rules, and one draw needn't show every extreme that they name: `dest`: every device sends exactly 32 blocks to each gy index. `elem`: on every owning device, each of its 128 elements receives exactly one block.
All inputs are finite; a program needn't handle non-finite values.
Results may differ from a plain program's by a relative error of at most 0.0003.
Values sent between devices are 32-bit elements; how exact they have to be, the bound alone decides.
A program may use at most 128 MiB of HBM per device.

v0:
```python
import functools

import jax
import jax.numpy as jnp
from jax import lax
from jax.experimental import pallas as pl
from jax.experimental.pallas import tpu as pltpu
from jax.sharding import PartitionSpec as P

GLL = (
    -1.0,
    -0.8717401485096066,
    -0.5917001814331423,
    -0.2092992179024789,
    0.2092992179024789,
    0.5917001814331423,
    0.8717401485096066,
    1.0,
)
SHARPNESS = 8.0
MESH = pl.DeviceIdType.MESH
F32 = jnp.float32
BF16 = jnp.bfloat16
I32 = jnp.int32
ROW = tuple((i % 2) * 4 + i // 2 for i in range(8))


def norm_consts():
    out = []
    for i in range(8):
        p = 1.0
        for m in range(8):
            if m != i:
                p *= GLL[i] - GLL[m]
        out.append(1.0 / p)
    return out


NORM = norm_consts()


def lagrange_all(x):
    d = [x - q for q in GLL]
    pre = [None] * 8
    suf = [None] * 8
    for i in range(1, 8):
        pre[i] = d[i - 1] if i == 1 else pre[i - 1] * d[i - 1]
    for i in range(6, -1, -1):
        suf[i] = d[i + 1] if i == 6 else suf[i + 1] * d[i + 1]
    out = []
    for i in range(8):
        if i == 0:
            v = suf[0]
        elif i == 7:
            v = pre[7]
        else:
            v = pre[i] * suf[i]
        out.append(v * NORM[i])
    return out


def gauss_all(x):
    return [jnp.exp(-SHARPNESS * (q - x) * (q - x)) for q in GLL]


def split_bf16(x):
    hi = x.astype(BF16)
    lo = (x - hi.astype(F32)).astype(BF16)
    return hi, lo


def rolled(x, by, axis):
    size = x.shape[axis]
    by = by % size
    if by == 0:
        return x
    return pltpu.roll(x, by, axis)


def kernel(
    field, pos, vel, coef, counts, dest, elem,
    drag_out, src_out,
    send, recv, lab_send, lab_recv, perm_v, perm_s, gt_v, fbuf, lag, gau, fluid, drag_s, ret,
    tot, gsend, grecv, ysend, yrecv,
    sm_sem, lab_ss, lab_rs, dat_ss, dat_rs, ret_ss, ret_rs, gm_ss, gm_rs, gp_ss, gp_rs, y_ss, y_rs,
):
    gx = lax.axis_index("gx")
    me = lax.axis_index("gy")
    n_gx = lax.axis_size("gx")
    n_gy = lax.axis_size("gy")
    has_prev = gx > 0
    has_next = gx < n_gx - 1
    has_lo = me > 0
    has_hi = me < n_gy - 1

    bar = pltpu.get_barrier_semaphore()
    for k in (1, 2, 3):
        pl.semaphore_signal(bar, inc=1, device_id={"gy": lax.rem(me + k, 4)}, device_id_type=MESH)

    @pl.when(has_prev)
    def _():
        pl.semaphore_signal(bar, inc=1, device_id={"gx": gx - 1}, device_id_type=MESH)

    @pl.when(has_next)
    def _():
        pl.semaphore_signal(bar, inc=1, device_id={"gx": gx + 1}, device_id_type=MESH)

    sub = lax.broadcasted_iota(I32, (128, 128), 0)
    lane = lax.broadcasted_iota(I32, (128, 128), 1)
    d_row = dest[...]
    d_b = jnp.broadcast_to(d_row, (128, 128))
    d_t = d_b.T
    before = jnp.where((d_b == d_t) & (sub < lane), 1, 0)
    rank = jnp.sum(before, axis=0, keepdims=True)
    place = d_row * 32 + rank
    p_t = jnp.broadcast_to(place, (128, 128)).T
    e_t = jnp.broadcast_to(elem[...], (128, 128)).T
    perm_v[0:1, :] = jnp.max(jnp.where(p_t == lane, sub, 0), axis=0, keepdims=True)
    perm_v[1:2, :] = d_row * 96 + rank
    to_smem = pltpu.make_async_copy(perm_v, perm_s, sm_sem.at[0])
    to_smem.start()
    mine = (lane >= me * 32) & (lane < me * 32 + 32)
    for k in range(4):
        d = lax.rem(me + k, 4)
        target = lane + (d - me) * 32
        row = jnp.max(jnp.where((p_t == target) & mine, e_t, 0), axis=0, keepdims=True)
        if k == 0:
            lab_recv[me] = row
        else:
            lab_send[k] = row

    pl.semaphore_wait(bar, 3 + (gx + n_gx - 1) // n_gx + (2 * n_gx - 2 - gx) // n_gx)

    def lab_copy(k):
        return pltpu.make_async_remote_copy(
            src_ref=lab_send.at[k], dst_ref=lab_recv.at[me],
            send_sem=lab_ss.at[k], recv_sem=lab_rs.at[lax.rem(4 - k, 4)],
            device_id={"gy": lax.rem(me + k, 4)}, device_id_type=MESH)

    def dat_copy(k):
        return pltpu.make_async_remote_copy(
            src_ref=send.at[k], dst_ref=recv.at[me],
            send_sem=dat_ss.at[k], recv_sem=dat_rs.at[lax.rem(4 - k, 4)],
            device_id={"gy": lax.rem(me + k, 4)}, device_id_type=MESH)

    def ret_copy(k):
        s = lax.rem(me + k, 4)
        return pltpu.make_async_remote_copy(
            src_ref=drag_s.at[pl.ds(pl.multiple_of(s * 96, 96), 96)],
            dst_ref=ret.at[pl.ds(pl.multiple_of(me * 96, 96), 96)],
            send_sem=ret_ss.at[k], recv_sem=ret_rs.at[lax.rem(4 - k, 4)],
            device_id={"gy": s}, device_id_type=MESH)

    for k in (2, 1, 3):
        lab_copy(k).start()
    to_smem.wait()

    slot_lane = lax.broadcasted_iota(I32, (1, 128), 1)

    def pack(dst, at, d):
        def step(g, _):
            for u in range(8):
                m = g * 8 + u
                b = perm_s[0, d * 32 + m]
                live = slot_lane < counts[b]
                c2 = coef[b]
                for c in range(3):
                    dst[at, pl.ds(c * 32 + m, 1), :] = pos[c, pl.ds(b, 1), :]
                    dst[at, pl.ds(96 + c * 32 + m, 1), :] = vel[c, pl.ds(b, 1), :]
                dst[at, pl.ds(192 + m, 1), :] = jnp.where(live, c2[0:1], 0.0)
                dst[at, pl.ds(224 + m, 1), :] = c2[1:2]
            return 0

        lax.fori_loop(0, 4, step, 0)

    def pack_and_send(q, _):
        k = 2 - q + 3 * (q // 2)
        pack(send, k, lax.rem(me + k, 4))
        dat_copy(k).start()
        return 0

    lax.fori_loop(0, 3, pack_and_send, 0)
    pack(recv, me, me)

    half = lax.broadcasted_iota(I32, (16, 128), 1) < 64

    def spread_field(n, _):
        c = n // 8
        ex = lax.rem(n // 4, 2)
        ey = lax.rem(n, 4)
        base = (ex * 4 + ey) * 16 * 24 + c * 8
        for t in range(4):
            x = field[c, ex, ey, :, t * 128:(t + 1) * 128].astype(F32)
            y = pltpu.roll(x, 64, 1)
            fbuf[pl.ds(base + t, 16, stride=24), :] = jnp.where(half, x, y)
            fbuf[pl.ds(base + 4 + t, 16, stride=24), :] = jnp.where(half, y, x)
        return 0

    lax.fori_loop(0, 24, spread_field, 0)

    for k in (1, 3, 2):
        lab_copy(k).wait()
    labels = lab_recv[0] + lab_recv[1] + lab_recv[2] + lab_recv[3]
    g_t = jnp.broadcast_to(labels, (128, 128)).T
    gt_v[...] = g_t
    inv = jnp.max(jnp.where(g_t == lane, sub, 0), axis=0, keepdims=True)
    perm_v[2:3, :] = labels
    perm_v[3:4, :] = inv
    perm_v[4:5, :] = (inv // 32) * 96 + lax.rem(inv, 32)
    to_smem = pltpu.make_async_copy(perm_v, perm_s, sm_sem.at[0])
    to_smem.start()
    to_smem.wait()

    hp = jnp.where(has_prev, 1.0, 0.0).astype(F32)
    hn = jnp.where(has_next, 1.0, 0.0).astype(F32)

    def chunk(q, _):
        k = lax.rem((q * q + q) // 2, 4)
        s = lax.rem(me + k, 4)

        @pl.when(q > 0)
        def _():
            dat_copy(lax.rem(4 - k, 4)).wait_recv()

        def bulk(g, _):
            first = s * 32 + g * 8

            def rows_of(r):
                return recv[s, pl.ds(pl.multiple_of(r * 32 + g * 8, 8), 8), :]

            def put(ref, kind, row, v):
                ref[kind, pl.ds(first * 8 + row, 8, stride=8), :] = v

            r, sc, tc = rows_of(0), rows_of(1), rows_of(2)
            lr, ls, lt = lagrange_all(r), lagrange_all(sc), lagrange_all(tc)
            for i in range(8):
                put(lag, 0, ROW[i], lr[i])
                put(lag, 1, i, ls[i])
                put(lag, 2, i, lt[i])
            ex0 = gt_v[pl.ds(pl.multiple_of(first, 8), 8), :] < 64
            own, minus, plus = gauss_all(r), gauss_all(r + 2.0), gauss_all(r - 2.0)
            zero = jnp.zeros_like(r)
            for i in range(8):
                o, p, m, x = own[i], plus[i], minus[i], zero
                if i == 0:
                    o = o + jnp.where(ex0, hp * minus[7], minus[7])
                    p = p + own[7]
                    x = jnp.where(ex0, plus[7], 0.0)
                if i == 7:
                    o = o + jnp.where(ex0, plus[0], hn * plus[0])
                    m = m + own[0]
                    x = jnp.where(ex0, 0.0, minus[0])
                put(gau, 0, ROW[i], o)
                put(gau, 1, ROW[i], p)
                put(gau, 2, ROW[i], m)
                put(gau, 3, ROW[i], x)
            gs, gt = gauss_all(sc), gauss_all(tc)
            for i in range(8):
                put(gau, 4, i, gs[i])
                put(gau, 5, i, gt[i])
            return 0

        lax.fori_loop(0, 4, bulk, 0)

        def interp(g, _):
            for u in range(4):
                slot = s * 32 + g * 4 + u
                e = perm_s[2, slot]
                f = fbuf[pl.ds(e * 24, 24), :].astype(BF16)
                at = pl.multiple_of(slot * 8, 8)
                lt = lag[2, pl.ds(at, 8), :]
                ls = lag[1, pl.ds(at, 8), :]
                plane = jnp.concatenate([ls[j:j + 1] * lt for j in range(8)], axis=0)
                hi, lo = split_bf16(plane)
                out = jnp.dot(f, jnp.concatenate([hi, lo], axis=0), preferred_element_type=F32)
                lr = lag[0, pl.ds(at, 8), :]
                for c in range(3):
                    fluid[c, pl.ds(slot, 1), :] = jnp.sum(out[8 * c:8 * c + 8] * lr, axis=0, keepdims=True)
            return 0

        lax.fori_loop(0, 8, interp, 0)

        rel = []
        for c in range(3):
            rel.append(fluid[c, pl.ds(pl.multiple_of(s * 32, 32), 32), :]
                       - recv[s, 96 + c * 32:128 + c * 32, :])
        speed = jnp.sqrt(rel[0] * rel[0] + rel[1] * rel[1] + rel[2] * rel[2])
        reynolds = jnp.maximum(recv[s, 224:256, :] * speed, 1e-30)
        factor = recv[s, 192:224, :] * (1.0 + 0.15 * jnp.exp(0.687 * jnp.log(reynolds)))
        for c in range(3):
            drag_s[pl.ds(pl.multiple_of(s * 96 + c * 32, 32), 32), :] = factor * rel[c]

        @pl.when(q > 0)
        def _():
            ret_copy(k).start()
        return 0

    lax.fori_loop(0, 4, chunk, 0)
    own_rows = pl.ds(pl.multiple_of(me * 96, 96), 96)
    ret[own_rows, :] = drag_s[own_rows, :]

    half8 = lax.broadcasted_iota(I32, (8, 128), 1) < 64

    def gm_copy(ey):
        return pltpu.make_async_remote_copy(
            src_ref=gsend.at[0, ey], dst_ref=grecv.at[0, ey], send_sem=gm_ss.at[ey], recv_sem=gm_rs.at[ey],
            device_id={"gx": gx - 1}, device_id_type=MESH)

    def gp_copy(ey):
        return pltpu.make_async_remote_copy(
            src_ref=gsend.at[1, ey], dst_ref=grecv.at[1, ey], send_sem=gp_ss.at[ey], recv_sem=gp_rs.at[ey],
            device_id={"gx": gx + 1}, device_id_type=MESH)

    def weights(slot, drow, order):
        at = slot * 8
        gs = gau[4, pl.ds(at, 8), :]
        gt = gau[5, pl.ds(at, 8), :]
        plane = jnp.concatenate([gs[j:j + 1] * gt for j in range(8)], axis=0)
        hi, lo = split_bf16(plane)
        rhs = jnp.concatenate([hi, lo], axis=0)
        d = [jnp.broadcast_to(-drag_s[pl.ds(drow + c * 32, 1), :], (8, 128)) for c in range(3)]
        w = [gau[n, pl.ds(at, 8), :] for n in order]
        lhs = jnp.concatenate([a * d[c] for a in w for c in range(3)], axis=0)
        lhi, llo = split_bf16(lhs)
        return rhs, lhi, llo

    def deposit_row(q, _):
        ey = lax.rem(3 * q, 4)

        def pair_group(g, _):
            for u in range(2):
                ez = g * 2 + u
                e0 = ey * 16 + ez
                e1 = 64 + e0
                r0, h0, l0 = weights(perm_s[3, e0], perm_s[4, e0], (0, 1, 2, 3))
                r1, h1, l1 = weights(perm_s[3, e1], perm_s[4, e1], (2, 0, 3, 1))
                lhs = jnp.concatenate(
                    [jnp.concatenate([h0, h1], axis=1), jnp.concatenate([l0, l1], axis=1)], axis=0)
                rhs = jnp.concatenate([r0, r1], axis=1)
                out = lax.dot_general(lhs, rhs, (((1,), (1,)), ((), ())), preferred_element_type=F32)
                z = out[0:96] + out[96:192]
                z = z + pltpu.roll(z, 64, 1)
                ezh = ez // 8
                ezl = lax.rem(ez, 8)
                for o in range(4):
                    for c in range(3):
                        v = z[(o * 3 + c) * 8:(o * 3 + c) * 8 + 8]
                        v = jnp.where(half8, v, pltpu.roll(v, 4, 0))[0:4]
                        if o < 2:
                            tot[c, o, ey, pl.ds(ezh * 32 + ezl, 4, stride=8), :] = v
                        else:
                            gsend[o - 2, ey, c, pl.ds(ezh * 32 + ezl, 4, stride=8), :] = v
            return 0

        lax.fori_loop(0, 8, pair_group, 0)

        @pl.when(has_prev)
        def _():
            gm_copy(ey).start()

        @pl.when(has_next)
        def _():
            gp_copy(ey).start()
        return 0

    lax.fori_loop(0, 4, deposit_row, 0)

    for k in (1, 3, 2):
        ret_copy(k).wait()

    def unpack(g, _):
        for u in range(8):
            b = g * 8 + u
            row = perm_s[1, b]
            for c in range(3):
                drag_out[c, pl.ds(b, 1), :] = ret[pl.ds(row + c * 32, 1), :]
        return 0

    lax.fori_loop(0, 16, unpack, 0)

    half32 = lax.broadcasted_iota(I32, (8, 128), 1) < 64

    def add_ghost(q, _):
        ey = lax.rem(3 * q, 4)

        @pl.when(has_next)
        def _():
            gm_copy(ey).wait_recv()

        @pl.when(jnp.logical_not(has_next))
        def _():
            grecv[0, ey] = jnp.zeros((3, 64, 128), F32)

        @pl.when(has_prev)
        def _():
            gp_copy(ey).wait_recv()

        @pl.when(jnp.logical_not(has_prev))
        def _():
            grecv[1, ey] = jnp.zeros((3, 64, 128), F32)

        for c in range(3):
            for h in range(2):
                for t in range(4):
                    rows = slice(h * 32 + t * 8, h * 32 + t * 8 + 8)
                    up = grecv[0, ey, c, rows, :]
                    down = grecv[1, ey, c, rows, :]
                    if t == 0:
                        far = pltpu.roll(grecv[1, ey, c, h * 32 + 24:h * 32 + 32, :], 64, 1)
                        up = up + jnp.where(half32, far, 0.0)
                    if t == 3:
                        far = pltpu.roll(grecv[0, ey, c, h * 32:h * 32 + 8, :], 64, 1)
                        down = down + jnp.where(half32, 0.0, far)
                    tot[c, 0, ey, rows, :] = tot[c, 0, ey, rows, :] + down
                    tot[c, 1, ey, rows, :] = tot[c, 1, ey, rows, :] + up
        return 0

    lax.fori_loop(0, 2, add_ghost, 0)

    lane8 = lax.broadcasted_iota(I32, (8, 128), 1)
    j8 = lax.rem(lane8 // 8, 8)
    for c in range(3):
        for h in range(2):
            lo_face = jnp.zeros((8, 128), F32)
            hi_face = jnp.zeros((8, 128), F32)
            for ex in range(2):
                for t in range(4):
                    n = ex * 4 + t
                    rows = slice(h * 32 + t * 8, h * 32 + t * 8 + 8)
                    lo_face = jnp.where(j8 == n, rolled(tot[c, ex, 0, rows, :], 8 * n, 1), lo_face)
                    hi_face = jnp.where(j8 == n, rolled(tot[c, ex, 3, rows, :], 8 * n - 56, 1), hi_face)
            ysend[0, (c * 2 + h) * 8:(c * 2 + h) * 8 + 8, :] = lo_face
            ysend[1, (c * 2 + h) * 8:(c * 2 + h) * 8 + 8, :] = hi_face

    def y_copy(way):
        return pltpu.make_async_remote_copy(
            src_ref=ysend.at[way], dst_ref=yrecv.at[way], send_sem=y_ss.at[way], recv_sem=y_rs.at[way],
            device_id={"gy": me - 1 if way == 0 else me + 1}, device_id_type=MESH)

    @pl.when(has_lo)
    def _():
        y_copy(0).start()

    @pl.when(has_hi)
    def _():
        y_copy(1).start()

    lax.fori_loop(2, 4, add_ghost, 0)

    @pl.when(has_hi)
    def _():
        y_copy(0).wait_recv()

    @pl.when(jnp.logical_not(has_hi))
    def _():
        yrecv[0] = jnp.zeros((48, 128), F32)

    @pl.when(has_lo)
    def _():
        y_copy(1).wait_recv()

    @pl.when(jnp.logical_not(has_lo))
    def _():
        yrecv[1] = jnp.zeros((48, 128), F32)

    lane16 = lax.broadcasted_iota(I32, (16, 128), 1)
    row16 = lax.broadcasted_iota(I32, (16, 128), 0)
    j16 = lax.rem(lane16 // 8, 8)
    k16 = lax.rem(lane16, 8)
    z_up = (k16 == 7) & (row16 < 15)
    z_down = (k16 == 0) & (row16 > 0)

    def finish(c, _):
        for ex in range(2):
            for t in range(4):
                n = ex * 4 + t
                lo_rows = slice(t * 8, t * 8 + 8)
                hi_rows = slice(32 + t * 8, 32 + t * 8 + 8)
                x = [jnp.concatenate([tot[c, ex, ey, lo_rows, :], tot[c, ex, ey, hi_rows, :]], axis=0)
                     for ey in range(4)]
                face = pl.ds(pl.multiple_of(c * 16, 16), 16)
                from_hi = rolled(yrecv[0, face, :], 56 - 8 * n, 1)
                from_lo = rolled(yrecv[1, face, :], -8 * n, 1)
                for ey in range(4):
                    nxt = from_hi if ey == 3 else pltpu.roll(x[ey + 1], 56, 1)
                    prv = from_lo if ey == 0 else pltpu.roll(x[ey - 1], 72, 1)
                    y = x[ey] + jnp.where(j16 == 7, nxt, jnp.where(j16 == 0, prv, 0.0))
                    above = pltpu.roll(pltpu.roll(y, 7, 1), 15, 0)
                    below = pltpu.roll(pltpu.roll(y, 121, 1), 1, 0)
                    src_out[c, ex, ey, :, t * 128:(t + 1) * 128] = y + jnp.where(
                        z_up, above, jnp.where(z_down, below, 0.0))
        return 0

    lax.fori_loop(0, 3, finish, 0)

    for k in (1, 2, 3):
        dat_copy(k).wait_send()

    for ey in range(4):
        @pl.when(has_prev)
        def _():
            gm_copy(ey).wait_send()

        @pl.when(has_next)
        def _():
            gp_copy(ey).wait_send()

    @pl.when(has_lo)
    def _():
        y_copy(0).wait_send()

    @pl.when(has_hi)
    def _():
        y_copy(1).wait_send()


def body(velocity, part_pos, part_vel, part_coef, counts, dest, elem):
    vm = pl.BlockSpec(memory_space=pltpu.VMEM)
    sm = pl.BlockSpec(memory_space=pltpu.SMEM)
    dma = pltpu.SemaphoreType.DMA
    drag, source = pl.pallas_call(
        kernel,
        out_shape=(
            jax.ShapeDtypeStruct((3, 128, 128), F32),
            jax.ShapeDtypeStruct(velocity.shape, F32),
        ),
        in_specs=[vm, vm, vm, vm, sm, vm, vm],
        out_specs=(vm, vm),
        scratch_shapes=[
            pltpu.VMEM((4, 256, 128), F32),
            pltpu.VMEM((4, 256, 128), F32),
            pltpu.VMEM((4, 1, 128), I32),
            pltpu.VMEM((4, 1, 128), I32),
            pltpu.VMEM((8, 128), I32),
            pltpu.SMEM((8, 128), I32),
            pltpu.VMEM((128, 128), I32),
            pltpu.VMEM((3072, 128), F32),
            pltpu.VMEM((3, 1024, 128), F32),
            pltpu.VMEM((6, 1024, 128), F32),
            pltpu.VMEM((3, 128, 128), F32),
            pltpu.VMEM((384, 128), F32),
            pltpu.VMEM((384, 128), F32),
            pltpu.VMEM((3, 2, 4, 64, 128), F32),
            pltpu.VMEM((2, 4, 3, 64, 128), F32),
            pltpu.VMEM((2, 4, 3, 64, 128), F32),
            pltpu.VMEM((2, 48, 128), F32),
            pltpu.VMEM((2, 48, 128), F32),
            dma((1,)), dma((4,)), dma((4,)), dma((4,)), dma((4,)), dma((4,)), dma((4,)),
            dma((4,)), dma((4,)), dma((4,)), dma((4,)), dma((2,)), dma((2,)),
        ],
        compiler_params=pltpu.CompilerParams(
            collective_id=0, has_side_effects=True, vmem_limit_bytes=40 * 1024 * 1024),
    )(velocity, part_pos.transpose(1, 0, 2), part_vel.transpose(1, 0, 2), part_coef, counts,
      dest.reshape(1, 128), elem.reshape(1, 128))
    return drag.transpose(1, 0, 2), source


def solution(mesh):
    in_specs = (
        P(None, "gx", "gy", None, None),
        P(("gx", "gy"), None, None),
        P(("gx", "gy"), None, None),
        P(("gx", "gy"), None, None),
        P(("gx", "gy")),
        P(("gx", "gy")),
        P(("gx", "gy")),
    )
    out_specs = (P(("gx", "gy"), None, None), P(None, "gx", "gy", None, None))
    return jax.shard_map(body, mesh=mesh, in_specs=in_specs, out_specs=out_specs, check_vma=False)
```

profile of v0, /device:TPU:30, one launch (start us, length us, event | category | flops | bytes accessed | tf_op | source)
XLA Modules:
  0.0 42.1 jit_solution(13619595500564709380)
XLA Ops:
  0.6 0.0 copy-start.4
  0.6 0.0 copy-start.5
  0.7 0.0 copy-start.6
  0.7 0.6 %copy-done.4 = s32[128]{0:T(128)S(1)} copy-done((s32[128]{0:T(128)S(1)}, s32[128]{0:T(128)}, u32[]{:S(2)}) %copy-start.4) | copy-done | bytes 536
  1.3 0.0 copy-done.5
  1.3 0.0 copy-done.6
  1.3 0.0 copy-start
  1.3 1.0 %copy-done = bf16[3,2,4,16,512]{4,3,2,1,0:T(8,128)(2,1)S(1)} copy-done((bf16[3,2,4,16,512]{4,3,2,1,0:T(8,128)(2,1)S(1)}, bf16[3,2,4,16,512]{4,3,2,1,0:T(8,128)(2,1)}, u32[]{:S(2)}) %copy-start) | copy-done | bytes 393240
  2.3 0.0 copy-start.1
  2.3 0.9 %copy-done.1 = f32[128,3,128]{2,0,1:T(8,128)S(1)} copy-done((f32[128,3,128]{2,0,1:T(8,128)S(1)}, f32[128,3,128]{2,0,1:T(8,128)}, u32[]{:S(2)}) %copy-start.1) | copy-done | bytes 196632
  3.2 0.0 copy-start.2
  3.2 0.9 %copy-done.2 = f32[128,3,128]{2,0,1:T(8,128)S(1)} copy-done((f32[128,3,128]{2,0,1:T(8,128)S(1)}, f32[128,3,128]{2,0,1:T(8,128)}, u32[]{:S(2)}) %copy-start.2) | copy-done | bytes 196632
  4.2 0.0 copy-start.3
  4.2 0.9 %copy-done.3 = f32[128,2,128]{2,1,0:T(2,128)S(1)} copy-done((f32[128,2,128]{2,1,0:T(2,128)S(1)}, f32[128,2,128]{2,1,0:T(2,128)}, u32[]{:S(2)}) %copy-start.3) | copy-done | bytes 131096
  5.1 35.5 %shard_map.86 = (f32[3,128,128]{2,1,0:T(8,128)S(1)}, f32[3,2,4,16,512]{4,3,2,1,0:T(8,128)S(1)}) custom-call(bf16[3,2,4,16,512]{4,3,2,1,0:T(8,128)(2,1)S(1)} %copy-done, f32[3,128,128]{2,1,0:T(8,128)S(1)} %bitcast.6, f32[3,128,128]{2,1,0:T(8,128)S(1)} %bitcast.7, f32[128,2,128]{2,1,0:T(2,128)S(1)} %copy-done.3, s32[128]{0:T(128)S(1)} %copy-done.4, ...), custom_call_target="tpu_custom_call" | custom-call | tf_op jit(solution)/shard_map/pallas_call | solution.py:521
  40.6 0.7 %copy.11 = f32[128,3,128]{2,0,1:T(8,128)} copy(f32[128,3,128]{2,0,1:T(8,128)S(1)} %bitcast.5) | data formatting | bytes 393216
  41.2 0.9 %copy.12 = f32[3,2,4,16,512]{4,3,2,1,0:T(8,128)} copy(f32[3,2,4,16,512]{4,3,2,1,0:T(8,128)S(1)} %get-tuple-element.9) | data formatting | bytes 1572864
Async XLA Ops:
  0.6 0.7 %copy-start.4 = (s32[128]{0:T(128)S(1)}, s32[128]{0:T(128)}, u32[]{:S(2)}) copy-start(s32[128]{0:T(128)} %counts.1) | copy-start | bytes 1540
  0.6 0.7 %copy-start.5 = (s32[128]{0:T(128)S(1)}, s32[128]{0:T(128)}, u32[]{:S(2)}) copy-start(s32[128]{0:T(128)} %param.12) | copy-start | bytes 1540
  0.7 0.7 %copy-start.6 = (s32[128]{0:T(128)S(1)}, s32[128]{0:T(128)}, u32[]{:S(2)}) copy-start(s32[128]{0:T(128)} %param.13) | copy-start | bytes 1540
  1.3 1.0 %copy-start = (bf16[3,2,4,16,512]{4,3,2,1,0:T(8,128)(2,1)S(1)}, bf16[3,2,4,16,512]{4,3,2,1,0:T(8,128)(2,1)}, u32[]{:S(2)}) copy-start(bf16[3,2,4,16,512]{4,3,2,1,0:T(8,128)(2,1)} %field.1) | copy-start | bytes 1179652
  2.3 0.9 %copy-start.1 = (f32[128,3,128]{2,0,1:T(8,128)S(1)}, f32[128,3,128]{2,0,1:T(8,128)}, u32[]{:S(2)}) copy-start(f32[128,3,128]{2,0,1:T(8,128)} %param.8) | copy-start | bytes 589828
  3.2 0.9 %copy-start.2 = (f32[128,3,128]{2,0,1:T(8,128)S(1)}, f32[128,3,128]{2,0,1:T(8,128)}, u32[]{:S(2)}) copy-start(f32[128,3,128]{2,0,1:T(8,128)} %param.9) | copy-start | bytes 589828
  4.2 0.9 %copy-start.3 = (f32[128,2,128]{2,1,0:T(2,128)S(1)}, f32[128,2,128]{2,1,0:T(2,128)}, u32[]{:S(2)}) copy-start(f32[128,2,128]{2,1,0:T(2,128)} %coef.1) | copy-start | bytes 393220
where the time goes:
time: 42.3 us; the launch traced here: 42.1 us
  Pallas kernels  35.5 us (84%)
  local copies, waits for them, and re-layouts  5.97 us (14%)
  between operations  0.67 us (2%)
    pallas_call x1, Pallas kernels, body(): pl.pallas_call(kernel, out_shape=(jax.ShapeDtypeStruct((3, 128, 128), F32...  35.5 us
    unnamed x16, local copies, waits for them, and re-layouts  5.97 us

commit v1 on v0

--- a/solution.py
+++ b/solution.py
@@ -78,10 +78,11 @@
 
 
 def kernel(
-    field, pos, vel, coef, counts, dest, elem,
+    field_h, pos_h, vel_h, coef_h, counts_h, dest_h, elem_h,
     drag_out, src_out,
+    field, pos, vel, coef, counts, dest, elem, in_sem,
     send, recv, lab_send, lab_recv, perm_v, perm_s, gt_v, fbuf, lag, gau, fluid, drag_s, ret,
-    tot, gsend, grecv, ysend, yrecv,
+    tot, ztot, gsend, grecv, ysend, yrecv,
     sm_sem, lab_ss, lab_rs, dat_ss, dat_rs, ret_ss, ret_rs, gm_ss, gm_rs, gp_ss, gp_rs, y_ss, y_rs,
 ):
     gx = lax.axis_index("gx")
@@ -93,6 +94,15 @@
     has_lo = me > 0
     has_hi = me < n_gy - 1
 
+    ins = [
+        pltpu.make_async_copy(a, b, in_sem.at[n])
+        for n, (a, b) in enumerate((
+            (dest_h, dest), (elem_h, elem), (counts_h, counts), (pos_h, pos), (vel_h, vel), (coef_h, coef),
+            (field_h, field)))
+    ]
+    for copy in ins:
+        copy.start()
+
     bar = pltpu.get_barrier_semaphore()
     for k in (1, 2, 3):
         pl.semaphore_signal(bar, inc=1, device_id={"gy": lax.rem(me + k, 4)}, device_id_type=MESH)
@@ -107,6 +117,8 @@
 
     sub = lax.broadcasted_iota(I32, (128, 128), 0)
     lane = lax.broadcasted_iota(I32, (128, 128), 1)
+    ins[0].wait()
+    ins[1].wait()
     d_row = dest[...]
     d_b = jnp.broadcast_to(d_row, (128, 128))
     d_t = d_b.T
@@ -173,6 +185,9 @@
 
         lax.fori_loop(0, 4, step, 0)
 
+    for n in (2, 3, 4, 5):
+        ins[n].wait()
+
     def pack_and_send(q, _):
         k = 2 - q + 3 * (q // 2)
         pack(send, k, lax.rem(me + k, 4))
@@ -183,6 +198,8 @@
     pack(recv, me, me)
 
     half = lax.broadcasted_iota(I32, (16, 128), 1) < 64
+
+    ins[6].wait()
 
     def spread_field(n, _):
         c = n // 8
@@ -263,8 +280,8 @@
         lax.fori_loop(0, 4, bulk, 0)
 
         def interp(g, _):
-            for u in range(4):
-                slot = s * 32 + g * 4 + u
+            for u in range(32):
+                slot = s * 32 + g * 32 + u
                 e = perm_s[2, slot]
                 f = fbuf[pl.ds(e * 24, 24), :].astype(BF16)
                 at = pl.multiple_of(slot * 8, 8)
@@ -278,7 +295,7 @@
                     fluid[c, pl.ds(slot, 1), :] = jnp.sum(out[8 * c:8 * c + 8] * lr, axis=0, keepdims=True)
             return 0
 
-        lax.fori_loop(0, 8, interp, 0)
+        interp(0, 0)
 
         rel = []
         for c in range(3):
@@ -328,8 +345,8 @@
         ey = lax.rem(3 * q, 4)
 
         def pair_group(g, _):
-            for u in range(2):
-                ez = g * 2 + u
+            for u in range(16):
+                ez = g * 16 + u
                 e0 = ey * 16 + ez
                 e1 = 64 + e0
                 r0, h0, l0 = weights(perm_s[3, e0], perm_s[4, e0], (0, 1, 2, 3))
@@ -340,8 +357,7 @@
                 out = lax.dot_general(lhs, rhs, (((1,), (1,)), ((), ())), preferred_element_type=F32)
                 z = out[0:96] + out[96:192]
                 z = z + pltpu.roll(z, 64, 1)
-                ezh = ez // 8
-                ezl = lax.rem(ez, 8)
+                ezh, ezl = ez // 8, ez % 8
                 for o in range(4):
                     for c in range(3):
                         v = z[(o * 3 + c) * 8:(o * 3 + c) * 8 + 8]
@@ -352,7 +368,7 @@
                             gsend[o - 2, ey, c, pl.ds(ezh * 32 + ezl, 4, stride=8), :] = v
             return 0
 
-        lax.fori_loop(0, 8, pair_group, 0)
+        pair_group(0, 0)
 
         @pl.when(has_prev)
         def _():
@@ -378,7 +394,13 @@
 
     lax.fori_loop(0, 16, unpack, 0)
 
-    half32 = lax.broadcasted_iota(I32, (8, 128), 1) < 64
+    lane16 = lax.broadcasted_iota(I32, (16, 128), 1)
+    row16 = lax.broadcasted_iota(I32, (16, 128), 0)
+    j16 = lax.rem(lane16 // 8, 8)
+    half16 = lane16 < 64
+    k16 = lax.rem(lane16, 8)
+    z_up = (k16 == 7) & (row16 < 15)
+    z_down = (k16 == 0) & (row16 > 0)
 
     def add_ghost(q, _):
         ey = lax.rem(3 * q, 4)
@@ -399,20 +421,24 @@
         def _():
             grecv[1, ey] = jnp.zeros((3, 64, 128), F32)
 
+        def tile(ref, t):
+            return jnp.concatenate([ref[t * 8:t * 8 + 8, :], ref[32 + t * 8:40 + t * 8, :]], axis=0)
+
         for c in range(3):
-            for h in range(2):
-                for t in range(4):
-                    rows = slice(h * 32 + t * 8, h * 32 + t * 8 + 8)
-                    up = grecv[0, ey, c, rows, :]
-                    down = grecv[1, ey, c, rows, :]
-                    if t == 0:
-                        far = pltpu.roll(grecv[1, ey, c, h * 32 + 24:h * 32 + 32, :], 64, 1)
-                        up = up + jnp.where(half32, far, 0.0)
-                    if t == 3:
-                        far = pltpu.roll(grecv[0, ey, c, h * 32:h * 32 + 8, :], 64, 1)
-                        down = down + jnp.where(half32, 0.0, far)
-                    tot[c, 0, ey, rows, :] = tot[c, 0, ey, rows, :] + down
-                    tot[c, 1, ey, rows, :] = tot[c, 1, ey, rows, :] + up
+            for t in range(4):
+                up = tile(grecv.at[0, ey, c], t)
+                down = tile(grecv.at[1, ey, c], t)
+                if t == 0:
+                    up = up + jnp.where(half16, pltpu.roll(tile(grecv.at[1, ey, c], 3), 64, 1), 0.0)
+                if t == 3:
+                    down = down + jnp.where(half16, 0.0, pltpu.roll(tile(grecv.at[0, ey, c], 0), 64, 1))
+                for ex, ghost in ((0, down), (1, up)):
+                    y = tile(tot.at[c, ex, ey], t) + ghost
+                    above = pltpu.roll(pltpu.roll(y, 7, 1), 15, 0)
+                    below = pltpu.roll(pltpu.roll(y, 121, 1), 1, 0)
+                    y = y + jnp.where(z_up, above, jnp.where(z_down, below, 0.0))
+                    ztot[c, ex, ey, t * 8:t * 8 + 8, :] = y[:8]
+                    ztot[c, ex, ey, 32 + t * 8:40 + t * 8, :] = y[8:]
         return 0
 
     lax.fori_loop(0, 2, add_ghost, 0)
@@ -427,8 +453,8 @@
                 for t in range(4):
                     n = ex * 4 + t
                     rows = slice(h * 32 + t * 8, h * 32 + t * 8 + 8)
-                    lo_face = jnp.where(j8 == n, rolled(tot[c, ex, 0, rows, :], 8 * n, 1), lo_face)
-                    hi_face = jnp.where(j8 == n, rolled(tot[c, ex, 3, rows, :], 8 * n - 56, 1), hi_face)
+                    lo_face = jnp.where(j8 == n, rolled(ztot[c, ex, 0, rows, :], 8 * n, 1), lo_face)
+                    hi_face = jnp.where(j8 == n, rolled(ztot[c, ex, 3, rows, :], 8 * n - 56, 1), hi_face)
             ysend[0, (c * 2 + h) * 8:(c * 2 + h) * 8 + 8, :] = lo_face
             ysend[1, (c * 2 + h) * 8:(c * 2 + h) * 8 + 8, :] = hi_face
 
@@ -462,13 +488,6 @@
     @pl.when(jnp.logical_not(has_lo))
     def _():
         yrecv[1] = jnp.zeros((48, 128), F32)
-
-    lane16 = lax.broadcasted_iota(I32, (16, 128), 1)
-    row16 = lax.broadcasted_iota(I32, (16, 128), 0)
-    j16 = lax.rem(lane16 // 8, 8)
-    k16 = lax.rem(lane16, 8)
-    z_up = (k16 == 7) & (row16 < 15)
-    z_down = (k16 == 0) & (row16 > 0)
 
     def finish(c, _):
         for ex in range(2):
@@ -476,7 +495,7 @@
                 n = ex * 4 + t
                 lo_rows = slice(t * 8, t * 8 + 8)
                 hi_rows = slice(32 + t * 8, 32 + t * 8 + 8)
-                x = [jnp.concatenate([tot[c, ex, ey, lo_rows, :], tot[c, ex, ey, hi_rows, :]], axis=0)
+                x = [jnp.concatenate([ztot[c, ex, ey, lo_rows, :], ztot[c, ex, ey, hi_rows, :]], axis=0)
                      for ey in range(4)]
                 face = pl.ds(pl.multiple_of(c * 16, 16), 16)
                 from_hi = rolled(yrecv[0, face, :], 56 - 8 * n, 1)
@@ -484,11 +503,8 @@
                 for ey in range(4):
                     nxt = from_hi if ey == 3 else pltpu.roll(x[ey + 1], 56, 1)
                     prv = from_lo if ey == 0 else pltpu.roll(x[ey - 1], 72, 1)
-                    y = x[ey] + jnp.where(j16 == 7, nxt, jnp.where(j16 == 0, prv, 0.0))
-                    above = pltpu.roll(pltpu.roll(y, 7, 1), 15, 0)
-                    below = pltpu.roll(pltpu.roll(y, 121, 1), 1, 0)
-                    src_out[c, ex, ey, :, t * 128:(t + 1) * 128] = y + jnp.where(
-                        z_up, above, jnp.where(z_down, below, 0.0))
+                    src_out[c, ex, ey, :, t * 128:(t + 1) * 128] = x[ey] + jnp.where(
+                        j16 == 7, nxt, jnp.where(j16 == 0, prv, 0.0))
         return 0
 
     lax.fori_loop(0, 3, finish, 0)
@@ -516,7 +532,7 @@
 
 def body(velocity, part_pos, part_vel, part_coef, counts, dest, elem):
     vm = pl.BlockSpec(memory_space=pltpu.VMEM)
-    sm = pl.BlockSpec(memory_space=pltpu.SMEM)
+    hbm = pl.BlockSpec(memory_space=pltpu.HBM)
     dma = pltpu.SemaphoreType.DMA
     drag, source = pl.pallas_call(
         kernel,
@@ -524,9 +540,17 @@
             jax.ShapeDtypeStruct((3, 128, 128), F32),
             jax.ShapeDtypeStruct(velocity.shape, F32),
         ),
-        in_specs=[vm, vm, vm, vm, sm, vm, vm],
+        in_specs=[hbm] * 7,
         out_specs=(vm, vm),
         scratch_shapes=[
+            pltpu.VMEM((3, 2, 4, 16, 512), BF16),
+            pltpu.VMEM((3, 128, 128), F32),
+            pltpu.VMEM((3, 128, 128), F32),
+            pltpu.VMEM((128, 2, 128), F32),
+            pltpu.SMEM((128,), I32),
+            pltpu.VMEM((1, 128), I32),
+            pltpu.VMEM((1, 128), I32),
+            dma((7,)),
             pltpu.VMEM((4, 256, 128), F32),
             pltpu.VMEM((4, 256, 128), F32),
             pltpu.VMEM((4, 1, 128), I32),
@@ -541,6 +565,7 @@
             pltpu.VMEM((384, 128), F32),
             pltpu.VMEM((384, 128), F32),
             pltpu.VMEM((3, 2, 4, 64, 128), F32),
+            pltpu.VMEM((3, 2, 4, 64, 128), F32),
             pltpu.VMEM((2, 4, 3, 64, 128), F32),
             pltpu.VMEM((2, 4, 3, 64, 128), F32),
             pltpu.VMEM((2, 48, 128), F32),
@@ -549,7 +574,7 @@
             dma((4,)), dma((4,)), dma((4,)), dma((4,)), dma((2,)), dma((2,)),
         ],
         compiler_params=pltpu.CompilerParams(
-            collective_id=0, has_side_effects=True, vmem_limit_bytes=40 * 1024 * 1024),
+            collective_id=0, has_side_effects=True, vmem_limit_bytes=67043328),
     )(velocity, part_pos.transpose(1, 0, 2), part_vel.transpose(1, 0, 2), part_coef, counts,
       dest.reshape(1, 128), elem.reshape(1, 128))
     return drag.transpose(1, 0, 2), source

time: 42.3 us -> 30 us (0.71)
  the two profiles are of different devices: /device:TPU:30 before, /device:TPU:28 now
where the time goes in v1:
time: 30 us; the launch traced here: 29.8 us
  Pallas kernels  25.4 us (85%)
  local copies, waits for them, and re-layouts  3.7 us (12%)
  between operations  0.64 us (2%)
    pallas_call x1, Pallas kernels, body(): pl.pallas_call(kernel, out_shape=(jax.ShapeDtypeStruct((3, 128, 128), F32...  25.4 us
    unnamed x2, local copies, waits for them, and re-layouts  3.7 us

profile of v1, /device:TPU:28, one launch (start us, length us, event | category | flops | bytes accessed | tf_op | source)
XLA Modules:
  0.0 29.8 jit_solution(10561169911382018988)
XLA Ops:
  0.6 25.4 %shard_map.86 = (f32[3,128,128]{2,1,0:T(8,128)}, f32[3,2,4,16,512]{4,3,2,1,0:T(8,128)}) custom-call(bf16[3,2,4,16,512]{4,3,2,1,0:T(8,128)(2,1)} %field_h.1, f32[3,128,128]{2,1,0:T(8,128)} %bitcast.6, f32[3,128,128]{2,1,0:T(8,128)} %bitcast.7, f32[128,2,128]{2,1,0:T(2,128)} %coef_h.1, s32[128]{0:T(128)} %counts_h.1, s32[1,128]{1,0:T(1,128)} %bitcast.8, ...), custom_call_target="tpu_custom_call" | custom-call | tf_op jit(solution)/shard_map/pallas_call | solution.py:537
  26.1 1.6 %copy.11 = f32[128,3,128]{2,0,1:T(8,128)} copy(f32[128,3,128]{2,0,1:T(8,128)} %bitcast.5) | data formatting | bytes 393216
  27.7 2.1 %copy.12 = f32[3,2,4,16,512]{4,3,2,1,0:T(8,128)} copy(f32[3,2,4,16,512]{4,3,2,1,0:T(8,128)} %get-tuple-element.9) | data formatting | bytes 1572864

commit v2 on v1

--- a/solution.py
+++ b/solution.py
@@ -79,11 +79,11 @@
 
 def kernel(
     field_h, pos_h, vel_h, coef_h, counts_h, dest_h, elem_h,
-    drag_out, src_out,
-    field, pos, vel, coef, counts, dest, elem, in_sem,
+    drag_h, ztot_h, face_h,
+    field, pos, vel, coef, counts, dest, elem, in_sem, drag_out, out_sem,
     send, recv, lab_send, lab_recv, perm_v, perm_s, gt_v, fbuf, lag, gau, fluid, drag_s, ret,
     tot, ztot, gsend, grecv, ysend, yrecv,
-    sm_sem, lab_ss, lab_rs, dat_ss, dat_rs, ret_ss, ret_rs, gm_ss, gm_rs, gp_ss, gp_rs, y_ss, y_rs,
+    sm_sem, lab_ss, lab_rs, pos_ss, pos_rs, dat_ss, dat_rs, ret_ss, ret_rs, gm_ss, gm_rs, gp_ss, gp_rs, y_ss, y_rs,
 ):
     gx = lax.axis_index("gx")
     me = lax.axis_index("gy")
@@ -141,17 +141,21 @@
         else:
             lab_send[k] = row
 
-    pl.semaphore_wait(bar, 3 + (gx + n_gx - 1) // n_gx + (2 * n_gx - 2 - gx) // n_gx)
-
     def lab_copy(k):
         return pltpu.make_async_remote_copy(
             src_ref=lab_send.at[k], dst_ref=lab_recv.at[me],
             send_sem=lab_ss.at[k], recv_sem=lab_rs.at[lax.rem(4 - k, 4)],
             device_id={"gy": lax.rem(me + k, 4)}, device_id_type=MESH)
 
+    def pos_copy(k):
+        return pltpu.make_async_remote_copy(
+            src_ref=send.at[k, pl.ds(0, 96)], dst_ref=recv.at[me, pl.ds(0, 96)],
+            send_sem=pos_ss.at[k], recv_sem=pos_rs.at[lax.rem(4 - k, 4)],
+            device_id={"gy": lax.rem(me + k, 4)}, device_id_type=MESH)
+
     def dat_copy(k):
         return pltpu.make_async_remote_copy(
-            src_ref=send.at[k], dst_ref=recv.at[me],
+            src_ref=send.at[k, pl.ds(96, 160)], dst_ref=recv.at[me, pl.ds(96, 160)],
             send_sem=dat_ss.at[k], recv_sem=dat_rs.at[lax.rem(4 - k, 4)],
             device_id={"gy": lax.rem(me + k, 4)}, device_id_type=MESH)
 
@@ -163,13 +167,20 @@
             send_sem=ret_ss.at[k], recv_sem=ret_rs.at[lax.rem(4 - k, 4)],
             device_id={"gy": s}, device_id_type=MESH)
 
-    for k in (2, 1, 3):
-        lab_copy(k).start()
-    to_smem.wait()
-
     slot_lane = lax.broadcasted_iota(I32, (1, 128), 1)
 
-    def pack(dst, at, d):
+    def pack_pos(dst, at, d):
+        def step(g, _):
+            for u in range(8):
+                m = g * 8 + u
+                b = perm_s[0, d * 32 + m]
+                for c in range(3):
+                    dst[at, pl.ds(c * 32 + m, 1), :] = pos[c, pl.ds(b, 1), :]
+            return 0
+
+        lax.fori_loop(0, 4, step, 0)
+
+    def pack_rest(dst, at, d):
         def step(g, _):
             for u in range(8):
                 m = g * 8 + u
@@ -177,7 +188,6 @@
                 live = slot_lane < counts[b]
                 c2 = coef[b]
                 for c in range(3):
-                    dst[at, pl.ds(c * 32 + m, 1), :] = pos[c, pl.ds(b, 1), :]
                     dst[at, pl.ds(96 + c * 32 + m, 1), :] = vel[c, pl.ds(b, 1), :]
                 dst[at, pl.ds(192 + m, 1), :] = jnp.where(live, c2[0:1], 0.0)
                 dst[at, pl.ds(224 + m, 1), :] = c2[1:2]
@@ -185,17 +195,36 @@
 
         lax.fori_loop(0, 4, step, 0)
 
-    for n in (2, 3, 4, 5):
+    def third(q):
+        return 2 - q + 3 * (q // 2)
+
+    to_smem.wait()
+    ins[3].wait()
+
+    def pack_pos_to(q, _):
+        k = third(q)
+        pack_pos(send, k, lax.rem(me + k, 4))
+        return 0
+
+    lax.fori_loop(0, 3, pack_pos_to, 0)
+    pl.semaphore_wait(bar, 3 + (gx + n_gx - 1) // n_gx + (2 * n_gx - 2 - gx) // n_gx)
+
+    for k in (2, 1, 3):
+        lab_copy(k).start()
+    for k in (2, 1, 3):
+        pos_copy(k).start()
+    for n in (2, 4, 5):
         ins[n].wait()
 
     def pack_and_send(q, _):
-        k = 2 - q + 3 * (q // 2)
-        pack(send, k, lax.rem(me + k, 4))
+        k = third(q)
+        pack_rest(send, k, lax.rem(me + k, 4))
         dat_copy(k).start()
         return 0
 
     lax.fori_loop(0, 3, pack_and_send, 0)
-    pack(recv, me, me)
+    pack_pos(recv, me, me)
+    pack_rest(recv, me, me)
 
     half = lax.broadcasted_iota(I32, (16, 128), 1) < 64
 
@@ -237,7 +266,7 @@
 
         @pl.when(q > 0)
         def _():
-            dat_copy(lax.rem(4 - k, 4)).wait_recv()
+            pos_copy(lax.rem(4 - k, 4)).wait_recv()
 
         def bulk(g, _):
             first = s * 32 + g * 8
@@ -296,6 +325,17 @@
             return 0
 
         interp(0, 0)
+        return 0
+
+    lax.fori_loop(0, 4, chunk, 0)
+
+    def drags(q, _):
+        k = lax.rem((q * q + q) // 2, 4)
+        s = lax.rem(me + k, 4)
+
+        @pl.when(q > 0)
+        def _():
+            dat_copy(lax.rem(4 - k, 4)).wait_recv()
 
         rel = []
         for c in range(3):
@@ -312,7 +352,7 @@
             ret_copy(k).start()
         return 0
 
-    lax.fori_loop(0, 4, chunk, 0)
+    lax.fori_loop(0, 4, drags, 0)
     own_rows = pl.ds(pl.multiple_of(me * 96, 96), 96)
     ret[own_rows, :] = drag_s[own_rows, :]
 
@@ -394,6 +434,12 @@
 
     lax.fori_loop(0, 16, unpack, 0)
 
+    drag_done = pltpu.make_async_copy(drag_out, drag_h, out_sem.at[6])
+    drag_done.start()
+
+    def z_copy(ey):
+        return pltpu.make_async_copy(ztot.at[:, :, ey], ztot_h.at[:, :, ey], out_sem.at[ey])
+
     lane16 = lax.broadcasted_iota(I32, (16, 128), 1)
     row16 = lax.broadcasted_iota(I32, (16, 128), 0)
     j16 = lax.rem(lane16 // 8, 8)
@@ -439,6 +485,7 @@
                     y = y + jnp.where(z_up, above, jnp.where(z_down, below, 0.0))
                     ztot[c, ex, ey, t * 8:t * 8 + 8, :] = y[:8]
                     ztot[c, ex, ey, 32 + t * 8:40 + t * 8, :] = y[8:]
+        z_copy(ey).start()
         return 0
 
     lax.fori_loop(0, 2, add_ghost, 0)
@@ -489,27 +536,12 @@
     def _():
         yrecv[1] = jnp.zeros((48, 128), F32)
 
-    def finish(c, _):
-        for ex in range(2):
-            for t in range(4):
-                n = ex * 4 + t
-                lo_rows = slice(t * 8, t * 8 + 8)
-                hi_rows = slice(32 + t * 8, 32 + t * 8 + 8)
-                x = [jnp.concatenate([ztot[c, ex, ey, lo_rows, :], ztot[c, ex, ey, hi_rows, :]], axis=0)
-                     for ey in range(4)]
-                face = pl.ds(pl.multiple_of(c * 16, 16), 16)
-                from_hi = rolled(yrecv[0, face, :], 56 - 8 * n, 1)
-                from_lo = rolled(yrecv[1, face, :], -8 * n, 1)
-                for ey in range(4):
-                    nxt = from_hi if ey == 3 else pltpu.roll(x[ey + 1], 56, 1)
-                    prv = from_lo if ey == 0 else pltpu.roll(x[ey - 1], 72, 1)
-                    src_out[c, ex, ey, :, t * 128:(t + 1) * 128] = x[ey] + jnp.where(
-                        j16 == 7, nxt, jnp.where(j16 == 0, prv, 0.0))
-        return 0
-
-    lax.fori_loop(0, 3, finish, 0)
+    faces = [pltpu.make_async_copy(yrecv.at[way], face_h.at[way], out_sem.at[4 + way]) for way in range(2)]
+    for copy in faces:
+        copy.start()
 
     for k in (1, 2, 3):
+        pos_copy(k).wait_send()
         dat_copy(k).wait_send()
 
     for ey in range(4):
@@ -528,20 +560,45 @@
     @pl.when(has_hi)
     def _():
         y_copy(1).wait_send()
+    drag_done.wait()
+    for ey in range(4):
+        z_copy(ey).wait()
+    for copy in faces:
+        copy.wait()
+
+
+def finish(drag_in, ztot, yrecv, drag_out, src_out):
+    drag_out[...] = drag_in[...]
+    lane16 = lax.broadcasted_iota(I32, (16, 128), 1)
+    j16 = lax.rem(lane16 // 8, 8)
+    for ex in range(2):
+        for t in range(4):
+            n = ex * 4 + t
+            lo_rows = slice(t * 8, t * 8 + 8)
+            hi_rows = slice(32 + t * 8, 32 + t * 8 + 8)
+            x = [jnp.concatenate([ztot[0, ex, ey, lo_rows, :], ztot[0, ex, ey, hi_rows, :]], axis=0)
+                 for ey in range(4)]
+            from_hi = rolled(yrecv[0], 56 - 8 * n, 1)
+            from_lo = rolled(yrecv[1], -8 * n, 1)
+            for ey in range(4):
+                nxt = from_hi if ey == 3 else pltpu.roll(x[ey + 1], 56, 1)
+                prv = from_lo if ey == 0 else pltpu.roll(x[ey - 1], 72, 1)
+                src_out[0, ex, ey, :, t * 128:(t + 1) * 128] = x[ey] + jnp.where(
+                    j16 == 7, nxt, jnp.where(j16 == 0, prv, 0.0))
 
 
 def body(velocity, part_pos, part_vel, part_coef, counts, dest, elem):
-    vm = pl.BlockSpec(memory_space=pltpu.VMEM)
     hbm = pl.BlockSpec(memory_space=pltpu.HBM)
     dma = pltpu.SemaphoreType.DMA
-    drag, source = pl.pallas_call(
+    drag, ztot, face = pl.pallas_call(
         kernel,
         out_shape=(
             jax.ShapeDtypeStruct((3, 128, 128), F32),
-            jax.ShapeDtypeStruct(velocity.shape, F32),
+            jax.ShapeDtypeStruct((3, 2, 4, 64, 128), F32),
+            jax.ShapeDtypeStruct((2, 48, 128), F32),
         ),
         in_specs=[hbm] * 7,
-        out_specs=(vm, vm),
+        out_specs=(hbm, hbm, hbm),
         scratch_shapes=[
             pltpu.VMEM((3, 2, 4, 16, 512), BF16),
             pltpu.VMEM((3, 128, 128), F32),
@@ -550,6 +607,8 @@
             pltpu.SMEM((128,), I32),
             pltpu.VMEM((1, 128), I32),
             pltpu.VMEM((1, 128), I32),
+            dma((7,)),
+            pltpu.VMEM((3, 128, 128), F32),
             dma((7,)),
             pltpu.VMEM((4, 256, 128), F32),
             pltpu.VMEM((4, 256, 128), F32),
@@ -570,13 +629,31 @@
             pltpu.VMEM((2, 4, 3, 64, 128), F32),
             pltpu.VMEM((2, 48, 128), F32),
             pltpu.VMEM((2, 48, 128), F32),
-            dma((1,)), dma((4,)), dma((4,)), dma((4,)), dma((4,)), dma((4,)), dma((4,)),
+            dma((1,)), dma((4,)), dma((4,)), dma((4,)), dma((4,)), dma((4,)), dma((4,)), dma((4,)), dma((4,)),
             dma((4,)), dma((4,)), dma((4,)), dma((4,)), dma((2,)), dma((2,)),
         ],
         compiler_params=pltpu.CompilerParams(
             collective_id=0, has_side_effects=True, vmem_limit_bytes=67043328),
     )(velocity, part_pos.transpose(1, 0, 2), part_vel.transpose(1, 0, 2), part_coef, counts,
       dest.reshape(1, 128), elem.reshape(1, 128))
+    drag, source = pl.pallas_call(
+        finish,
+        grid=(3,),
+        in_specs=[
+            pl.BlockSpec((1, 128, 128), lambda c: (c, 0, 0)),
+            pl.BlockSpec((1, 2, 4, 64, 128), lambda c: (c, 0, 0, 0, 0)),
+            pl.BlockSpec((2, 16, 128), lambda c: (0, c, 0)),
+        ],
+        out_specs=(
+            pl.BlockSpec((1, 128, 128), lambda c: (c, 0, 0)),
+            pl.BlockSpec((1, 2, 4, 16, 512), lambda c: (c, 0, 0, 0, 0)),
+        ),
+        out_shape=(
+            jax.ShapeDtypeStruct((3, 128, 128), F32),
+            jax.ShapeDtypeStruct(velocity.shape, F32),
+        ),
+        compiler_params=pltpu.CompilerParams(vmem_limit_bytes=67043328),
+    )(drag, ztot, face)
     return drag.transpose(1, 0, 2), source
 
 

time: 30 us -> 26.7 us (0.89)
  the two profiles are of different devices: /device:TPU:28 before, /device:TPU:26 now
where the time goes in v2:
time: 26.7 us; the launch traced here: 26.5 us
  Pallas kernels  25.9 us (97%)
  between operations  0.64 us (2%)
    pallas_call x1, Pallas kernels, body(): pl.pallas_call(kernel, out_shape=(jax.ShapeDtypeStruct((3, 128, 128), F32...  22.7 us
    pallas_call x1, Pallas kernels, body(): pl.pallas_call(finish, grid=(3,), in_specs=[pl.BlockSpec((1, 128, 128), l...  3.22 us

profile of v2, /device:TPU:26, one launch (start us, length us, event | category | flops | bytes accessed | tf_op | source)
XLA Modules:
  0.0 26.5 jit_solution(11413059686597694746)
XLA Ops:
  0.6 22.7 %shard_map.86 = (f32[3,128,128]{2,1,0:T(8,128)}, f32[3,2,4,64,128]{4,3,2,1,0:T(8,128)}, f32[2,48,128]{2,1,0:T(8,128)}) custom-call(bf16[3,2,4,16,512]{4,3,2,1,0:T(8,128)(2,1)} %field_h.1, f32[3,128,128]{2,1,0:T(8,128)} %bitcast.5, f32[3,128,128]{2,1,0:T(8,128)} %bitcast.6, f32[128,2,128]{2,1,0:T(2,128)} %coef_h.1, s32[128]{0:T(128)} %counts_h.1, ...), custom_call_target="tpu_custom_call" | custom-call | tf_op jit(solution)/shard_map/pallas_call | solution.py:593
  23.3 3.2 %shard_map.87 = (f32[3,128,128]{2,1,0:T(8,128)}, f32[3,2,4,16,512]{4,3,2,1,0:T(8,128)}) custom-call(f32[3,128,128]{2,1,0:T(8,128)} %get-tuple-element.7.drag_in, f32[3,2,4,64,128]{4,3,2,1,0:T(8,128)} %get-tuple-element.8.ztot, f32[2,48,128]{2,1,0:T(8,128)} %get-tuple-element.9.yrecv), custom_call_target="tpu_custom_call" | custom-call | tf_op jit(solution)/shard_map/pallas_call | solution.py:639

commit v3 on v2

--- a/solution.py
+++ b/solution.py
@@ -567,24 +567,47 @@
         copy.wait()
 
 
-def finish(drag_in, ztot, yrecv, drag_out, src_out):
-    drag_out[...] = drag_in[...]
+def finish(drag_h, ztot_h, face_h, drag_o, src_o, drag, ztot, yrecv, src, in_sem, out_sem):
+    faces_in = pltpu.make_async_copy(face_h, yrecv, in_sem.at[6])
+    drag_in = pltpu.make_async_copy(drag_h, drag, in_sem.at[7])
+    drag_done = pltpu.make_async_copy(drag, drag_o, out_sem.at[6])
+
+    def z_in(n):
+        return pltpu.make_async_copy(ztot_h.at[n // 2, n % 2], ztot.at[n // 2, n % 2], in_sem.at[n])
+
+    def z_out(n):
+        return pltpu.make_async_copy(src.at[n // 2, n % 2], src_o.at[n // 2, n % 2], out_sem.at[n])
+
+    faces_in.start()
+    for n in range(6):
+        z_in(n).start()
+    drag_in.start()
     lane16 = lax.broadcasted_iota(I32, (16, 128), 1)
     j16 = lax.rem(lane16 // 8, 8)
-    for ex in range(2):
+    faces_in.wait()
+    for part in range(6):
+        c, ex = part // 2, part % 2
+        z_in(part).wait()
         for t in range(4):
             n = ex * 4 + t
             lo_rows = slice(t * 8, t * 8 + 8)
             hi_rows = slice(32 + t * 8, 32 + t * 8 + 8)
-            x = [jnp.concatenate([ztot[0, ex, ey, lo_rows, :], ztot[0, ex, ey, hi_rows, :]], axis=0)
+            x = [jnp.concatenate([ztot[c, ex, ey, lo_rows, :], ztot[c, ex, ey, hi_rows, :]], axis=0)
                  for ey in range(4)]
-            from_hi = rolled(yrecv[0], 56 - 8 * n, 1)
-            from_lo = rolled(yrecv[1], -8 * n, 1)
+            from_hi = rolled(yrecv[0, c * 16:c * 16 + 16, :], 56 - 8 * n, 1)
+            from_lo = rolled(yrecv[1, c * 16:c * 16 + 16, :], -8 * n, 1)
             for ey in range(4):
                 nxt = from_hi if ey == 3 else pltpu.roll(x[ey + 1], 56, 1)
                 prv = from_lo if ey == 0 else pltpu.roll(x[ey - 1], 72, 1)
-                src_out[0, ex, ey, :, t * 128:(t + 1) * 128] = x[ey] + jnp.where(
+                src[c, ex, ey, :, t * 128:(t + 1) * 128] = x[ey] + jnp.where(
                     j16 == 7, nxt, jnp.where(j16 == 0, prv, 0.0))
+        z_out(part).start()
+        if part == 1:
+            drag_in.wait()
+            drag_done.start()
+    for n in range(6):
+        z_out(n).wait()
+    drag_done.wait()
 
 
 def body(velocity, part_pos, part_vel, part_coef, counts, dest, elem):
@@ -638,20 +661,19 @@
       dest.reshape(1, 128), elem.reshape(1, 128))
     drag, source = pl.pallas_call(
         finish,
-        grid=(3,),
-        in_specs=[
-            pl.BlockSpec((1, 128, 128), lambda c: (c, 0, 0)),
-            pl.BlockSpec((1, 2, 4, 64, 128), lambda c: (c, 0, 0, 0, 0)),
-            pl.BlockSpec((2, 16, 128), lambda c: (0, c, 0)),
-        ],
-        out_specs=(
-            pl.BlockSpec((1, 128, 128), lambda c: (c, 0, 0)),
-            pl.BlockSpec((1, 2, 4, 16, 512), lambda c: (c, 0, 0, 0, 0)),
-        ),
+        in_specs=[hbm] * 3,
+        out_specs=(hbm, hbm),
         out_shape=(
             jax.ShapeDtypeStruct((3, 128, 128), F32),
             jax.ShapeDtypeStruct(velocity.shape, F32),
         ),
+        scratch_shapes=[
+            pltpu.VMEM((3, 128, 128), F32),
+            pltpu.VMEM((3, 2, 4, 64, 128), F32),
+            pltpu.VMEM((2, 48, 128), F32),
+            pltpu.VMEM(velocity.shape, F32),
+            dma((8,)), dma((7,)),
+        ],
         compiler_params=pltpu.CompilerParams(vmem_limit_bytes=67043328),
     )(drag, ztot, face)
     return drag.transpose(1, 0, 2), source

time: 26.7 us -> 26.1 us (0.978)
  Pallas kernels: 25.9 us -> 25.3 us
    pallas_call x1, Pallas kernels: 3.22 us -> 2.61 us  [body(): pl.pallas_call(finish, in_specs=[hbm] * 3, out_specs=(hbm, hbm), out_shap...]
where the time goes in v3:
time: 26.1 us; the launch traced here: 25.9 us
  Pallas kernels  25.3 us (97%)
  between operations  0.64 us (2%)
    pallas_call x1, Pallas kernels, body(): pl.pallas_call(kernel, out_shape=(jax.ShapeDtypeStruct((3, 128, 128), F32...  22.7 us
    pallas_call x1, Pallas kernels, body(): pl.pallas_call(finish, in_specs=[hbm] * 3, out_specs=(hbm, hbm), out_shap...  2.61 us

profile of v3, /device:TPU:26, one launch (start us, length us, event | category | flops | bytes accessed | tf_op | source)
XLA Modules:
  0.0 25.9 jit_solution(12107420566852749711)
XLA Ops:
  0.6 22.7 %shard_map.86 = (f32[3,128,128]{2,1,0:T(8,128)}, f32[3,2,4,64,128]{4,3,2,1,0:T(8,128)}, f32[2,48,128]{2,1,0:T(8,128)}) custom-call(bf16[3,2,4,16,512]{4,3,2,1,0:T(8,128)(2,1)} %field_h.1, f32[3,128,128]{2,1,0:T(8,128)} %bitcast.5, f32[3,128,128]{2,1,0:T(8,128)} %bitcast.6, f32[128,2,128]{2,1,0:T(2,128)} %coef_h.1, s32[128]{0:T(128)} %counts_h.1, ...), custom_call_target="tpu_custom_call" | custom-call | tf_op jit(solution)/shard_map/pallas_call | solution.py:616
  23.3 2.6 %shard_map.87 = (f32[3,128,128]{2,1,0:T(8,128)}, f32[3,2,4,16,512]{4,3,2,1,0:T(8,128)}) custom-call(f32[3,128,128]{2,1,0:T(8,128)} %get-tuple-element.7.drag_h, f32[3,2,4,64,128]{4,3,2,1,0:T(8,128)} %get-tuple-element.8.ztot_h, f32[2,48,128]{2,1,0:T(8,128)} %get-tuple-element.9.face_h), custom_call_target="tpu_custom_call" | custom-call | tf_op jit(solution)/shard_map/pallas_call | solution.py:662

commit v4 on v3

--- a/solution.py
+++ b/solution.py
@@ -211,7 +211,7 @@
 
     for k in (2, 1, 3):
         lab_copy(k).start()
-    for k in (2, 1, 3):
+    for k in (1, 3, 2):
         pos_copy(k).start()
     for n in (2, 4, 5):
         ins[n].wait()
@@ -573,13 +573,13 @@
     drag_done = pltpu.make_async_copy(drag, drag_o, out_sem.at[6])
 
     def z_in(n):
-        return pltpu.make_async_copy(ztot_h.at[n // 2, n % 2], ztot.at[n // 2, n % 2], in_sem.at[n])
+        return pltpu.make_async_copy(ztot_h.at[n], ztot.at[n], in_sem.at[n])
 
     def z_out(n):
-        return pltpu.make_async_copy(src.at[n // 2, n % 2], src_o.at[n // 2, n % 2], out_sem.at[n])
+        return pltpu.make_async_copy(src.at[n], src_o.at[n], out_sem.at[n])
 
     faces_in.start()
-    for n in range(6):
+    for n in range(3):
         z_in(n).start()
     drag_in.start()
     lane16 = lax.broadcasted_iota(I32, (16, 128), 1)
@@ -587,7 +587,8 @@
     faces_in.wait()
     for part in range(6):
         c, ex = part // 2, part % 2
-        z_in(part).wait()
+        if ex == 0:
+            z_in(c).wait()
         for t in range(4):
             n = ex * 4 + t
             lo_rows = slice(t * 8, t * 8 + 8)
@@ -601,11 +602,12 @@
                 prv = from_lo if ey == 0 else pltpu.roll(x[ey - 1], 72, 1)
                 src[c, ex, ey, :, t * 128:(t + 1) * 128] = x[ey] + jnp.where(
                     j16 == 7, nxt, jnp.where(j16 == 0, prv, 0.0))
-        z_out(part).start()
+        if ex == 1:
+            z_out(c).start()
         if part == 1:
             drag_in.wait()
             drag_done.start()
-    for n in range(6):
+    for n in range(3):
         z_out(n).wait()
     drag_done.wait()
 

time: 26.1 us -> 25.6 us (0.981)
  the two profiles are of different devices: /device:TPU:26 before, /device:TPU:1 now
where the time goes in v4:
time: 25.6 us; the launch traced here: 25.4 us
  Pallas kernels  24.8 us (97%)
  between operations  0.64 us (2%)
    pallas_call x1, Pallas kernels, body(): pl.pallas_call(kernel, out_shape=(jax.ShapeDtypeStruct((3, 128, 128), F32...  22.4 us
    pallas_call x1, Pallas kernels, body(): pl.pallas_call(finish, in_specs=[hbm] * 3, out_specs=(hbm, hbm), out_shap...  2.43 us

profile of v4, /device:TPU:1, one launch (start us, length us, event | category | flops | bytes accessed | tf_op | source)
XLA Modules:
  0.0 25.4 jit_solution(18245599980768837595)
XLA Ops:
  0.6 22.4 %shard_map.86 = (f32[3,128,128]{2,1,0:T(8,128)}, f32[3,2,4,64,128]{4,3,2,1,0:T(8,128)}, f32[2,48,128]{2,1,0:T(8,128)}) custom-call(bf16[3,2,4,16,512]{4,3,2,1,0:T(8,128)(2,1)} %field_h.1, f32[3,128,128]{2,1,0:T(8,128)} %bitcast.5, f32[3,128,128]{2,1,0:T(8,128)} %bitcast.6, f32[128,2,128]{2,1,0:T(2,128)} %coef_h.1, s32[128]{0:T(128)} %counts_h.1, ...), custom_call_target="tpu_custom_call" | custom-call | tf_op jit(solution)/shard_map/pallas_call | solution.py:618
  23.0 2.4 %shard_map.87 = (f32[3,128,128]{2,1,0:T(8,128)}, f32[3,2,4,16,512]{4,3,2,1,0:T(8,128)}) custom-call(f32[3,128,128]{2,1,0:T(8,128)} %get-tuple-element.7.drag_h, f32[3,2,4,64,128]{4,3,2,1,0:T(8,128)} %get-tuple-element.8.ztot_h, f32[2,48,128]{2,1,0:T(8,128)} %get-tuple-element.9.face_h), custom_call_target="tpu_custom_call" | custom-call | tf_op jit(solution)/shard_map/pallas_call | solution.py:664
